TPU v7x, 32 devices: a whole 2x2x4 slice. The times are simulated.
32 devices in a mesh: group: 8 (over y, x, core), head: 4 (over z).
Axes of the slice: x: 2, y: 2, z: 4, core: 2. Of those that a mesh axis runs over, the one named last changes fastest.
Arguments:
- hidden_in: bfloat16 [128, 2560], P('group'), may hold values from -6 to 6
- ssm_state: float32 [128, 80, 64, 128], P('group', 'head'), may hold values from -6 to 6
- conv_x_state: bfloat16 [128, 3, 5120], P('group', None, 'head'), may hold values from -6 to 6
- conv_bc_state: bfloat16 [128, 3, 256], P('group'), may hold values from -6 to 6
- token_ids: int32 [128], P('group'), may hold values from 0 to 25599
- ref_logits: bfloat16 [128, 25600], P('group', 'head'), may hold values from -15 to 350
- in_z: bfloat16 [2560, 5120], P('group', 'head'), may hold values from -0.125 to 0.125
- in_x: bfloat16 [2560, 5120], P('group', 'head'), may hold values from -0.125 to 0.125
- in_bc: bfloat16 [2560, 256], P('group'), may hold values from -0.125 to 0.125
- in_dt: bfloat16 [2560, 80], P('group', 'head'), may hold values from -0.125 to 0.125
- out_t: bfloat16 [2560, 5120], P('group', 'head'), may hold values from -0.078125 to 0.078125
- lm_head: bfloat16 [25600, 2560], P('head', 'group'), may hold values from -6 to 6
- conv_wx: float32 [4, 5120], P(None, 'head'), may hold values from -3 to 3
- conv_bx: float32 [5120], P('head'), may hold values from -1.5 to 1.5
- conv_wbc: float32 [4, 256], replicated, may hold values from -3 to 3
- conv_bbc: float32 [256], replicated, may hold values from -1.5 to 1.5
- dt_bias: float32 [80], P('head'), may hold values from -4 to -1
- a_log: float32 [80], P('head'), may hold values from 0 to 2.77
- skip_gain: float32 [80], P('head'), may hold values from 0.5 to 1.5
- norm_in: float32 [2560], replicated, may hold values from 0.5 to 1.5
- norm_gain: float32 [5120], P('head'), may hold values from 0.5 to 1.5
- final_gain: float32 [2560], replicated, may hold values from 0.5 to 1.5
Outputs:
- new_state: float32 [128, 80, 64, 128], P('group', 'head')
- divergence: float32 [128], P('group')
- token_logprob: float32 [128], P('group')
- roll_z: bfloat16 [2560, 5120], P(None, 'head')
- roll_x: bfloat16 [2560, 5120], P(None, 'head')
- roll_bc: bfloat16 [2560, 256], replicated
- roll_dt: bfloat16 [2560, 80], P(None, 'head')
- roll_out: bfloat16 [2560, 5120], P(None, 'head')
All inputs are finite; a program needn't handle non-finite values.
Results may differ from a plain program's by a relative error of at most 0.0102.
Values may be sent and summed in bfloat16 or wider, within the bound.
A program may use at most 128 MiB of HBM per device.

v0:
```python
import jax
import jax.numpy as jnp
from jax import lax
from jax.sharding import PartitionSpec as P

P_SIZE = 64
EPSILON = 1e-05


def rms_norm(values, gain):
    return values * lax.rsqrt(jnp.mean(values * values, axis=-1, keepdims=True) + EPSILON) * gain


def causal_conv(history, newest, taps, offset):
    window = jnp.concatenate([history, newest[:, None, :]], axis=1).astype(jnp.float32)
    return jax.nn.silu(jnp.sum(window * taps[None, :, :], axis=1) + offset)


def shards(
    hidden_in,
    ssm_state,
    conv_x_state,
    conv_bc_state,
    token_ids,
    ref_logits,
    in_z,
    in_x,
    in_bc,
    in_dt,
    out_t,
    lm_head,
    conv_wx,
    conv_bx,
    conv_wbc,
    conv_bbc,
    dt_bias,
    a_log,
    skip_gain,
    norm_in,
    norm_gain,
    final_gain,
):
    roll_z, roll_x, roll_bc, roll_dt, roll_out = (
        lax.all_gather(in_z, "group", axis=0, tiled=True),
        lax.all_gather(in_x, "group", axis=0, tiled=True),
        lax.all_gather(in_bc, "group", axis=0, tiled=True),
        lax.all_gather(in_dt, "group", axis=0, tiled=True),
        lax.all_gather(out_t, "group", axis=0, tiled=True),
    )
    stream_in = hidden_in.astype(jnp.float32)
    normed = rms_norm(stream_in, norm_in).astype(jnp.bfloat16)
    gate_branch = jnp.dot(normed, roll_z, preferred_element_type=jnp.float32).astype(jnp.bfloat16)
    x_branch = jnp.dot(normed, roll_x, preferred_element_type=jnp.float32).astype(jnp.bfloat16)
    bc_branch = jnp.dot(normed, roll_bc, preferred_element_type=jnp.float32).astype(jnp.bfloat16)
    step_raw = jnp.dot(normed, roll_dt, preferred_element_type=jnp.float32).astype(jnp.bfloat16)
    x_conv = causal_conv(conv_x_state, x_branch, conv_wx, conv_bx)
    bc_conv = causal_conv(conv_bc_state, bc_branch, conv_wbc, conv_bbc)
    state_size = bc_conv.shape[1] // 2
    b_vals = bc_conv[:, :state_size]
    c_vals = bc_conv[:, state_size:]
    step = jax.nn.softplus(step_raw.astype(jnp.float32) + dt_bias)
    decay = jnp.exp(-step * jnp.exp(a_log))
    seq_count = x_conv.shape[0]
    local_heads = a_log.shape[0]
    x_heads = x_conv.reshape(seq_count, local_heads, P_SIZE)
    inflow = (step[:, :, None] * x_heads)[:, :, :, None] * b_vals[:, None, None, :]
    new_state = decay[:, :, None, None] * ssm_state + inflow
    ssm_out = jnp.einsum("shpn,sn->shp", new_state, c_vals, precision=lax.Precision.HIGHEST)
    ssm_out = (ssm_out + skip_gain[None, :, None] * x_heads).reshape(
        seq_count, local_heads * P_SIZE
    )
    gated = ssm_out * jax.nn.silu(gate_branch.astype(jnp.float32))
    square_total = lax.psum(jnp.sum(gated * gated, axis=-1), "head")
    inner_width = gated.shape[1] * lax.axis_size("head")
    gated_out = (
        gated * lax.rsqrt(square_total / inner_width + EPSILON)[:, None] * norm_gain
    ).astype(jnp.bfloat16)
    partial_mix = lax.dot_general(
        gated_out, roll_out, (((1,), (1,)), ((), ())), preferred_element_type=jnp.float32
    )
    mixed = lax.psum(partial_mix, "head")
    final_hidden = rms_norm(stream_in + mixed, final_gain).astype(jnp.bfloat16)
    vocab_local = lm_head.shape[0]
    whole_rows = lax.all_to_all(lm_head, "group", split_axis=0, concat_axis=1, tiled=True)
    every_logits = lax.dot_general(
        lax.all_gather(final_hidden, "group", axis=0, tiled=True),
        whole_rows,
        (((1,), (1,)), ((), ())),
        preferred_element_type=jnp.float32,
    )
    logits = lax.all_to_all(every_logits, "group", split_axis=0, concat_axis=1, tiled=True)
    reference_rows = ref_logits.astype(jnp.float32)
    column_ids = lax.axis_index("head") * vocab_local + lax.broadcasted_iota(
        jnp.int32, (1, vocab_local), 1
    )
    picked_part = jnp.sum(jnp.where(column_ids == token_ids[:, None], logits, 0.0), axis=-1)
    roll_max, ref_max = lax.pmax(
        (jnp.max(logits, axis=-1), jnp.max(reference_rows, axis=-1)), "head"
    )
    ref_weights = jnp.exp(reference_rows - ref_max[:, None])
    roll_sum, ref_sum, cross_sum, picked = lax.psum(
        (
            jnp.sum(jnp.exp(logits - roll_max[:, None]), axis=-1),
            jnp.sum(ref_weights, axis=-1),
            jnp.sum(ref_weights * (reference_rows - logits), axis=-1),
            picked_part,
        ),
        "head",
    )
    lse_roll = roll_max + jnp.log(roll_sum)
    lse_ref = ref_max + jnp.log(ref_sum)
    divergence = cross_sum / ref_sum - lse_ref + lse_roll
    token_logprob = picked - lse_roll
    return (new_state, divergence, token_logprob, roll_z, roll_x, roll_bc, roll_dt, roll_out)


def solution(mesh):
    return jax.shard_map(
        shards,
        mesh=mesh,
        in_specs=(
            P("group", None),
            P("group", "head", None, None),
            P("group", None, "head"),
            P("group", None, None),
            P("group"),
            P("group", "head"),
            P("group", "head"),
            P("group", "head"),
            P("group", None),
            P("group", "head"),
            P("group", "head"),
            P("head", "group"),
            P(None, "head"),
            P("head"),
            P(),
            P(),
            P("head"),
            P("head"),
            P("head"),
            P(),
            P("head"),
            P(),
        ),
        out_specs=(
            P("group", "head", None, None),
            P("group"),
            P("group"),
            P(None, "head"),
            P(None, "head"),
            P(),
            P(None, "head"),
            P(None, "head"),
        ),
        check_vma=False,
    )
```

profile of v0, /device:TPU:0, one launch (start us, length us, event | category | flops | bytes accessed | tf_op | source)
XLA Modules:
  0.0 324.4 jit_solution(13487269814347778549)
XLA Ops:
  7.2 0.7 all-gather.8.cloned.1.call-update
  7.9 0.7 all-gather.6.cloned.1.call-update
  8.7 0.7 all-gather.10.cloned.1.call-update
  9.4 0.5 all-gather.12.cloned.1.call-update
  10.0 10.6 %all_to_all.26 = bf16[8,800,320]{1,0,2:T(8,128)(2,1)} reshape(bf16[6400,320]{0,1:T(8,128)(2,1)} %param.33) | data formatting | bytes 8192000 | tf_op jit(solution)/shard_map/all_to_all | solution.py:84
  20.5 5.2 %copy.40 = bf16[8,800,320]{1,2,0:T(8,128)(2,1)} copy(bf16[8,800,320]{1,0,2:T(8,128)(2,1)} %all_to_all.26) | data formatting | bytes 8192000 | tf_op jit(solution)/shard_map/all_to_all | solution.py:84
  25.8 5.4 %all-to-all-start = ((bf16[8,800,320]{1,2,0:T(8,128)(2,1)}), bf16[8,800,320]{1,2,0:T(8,128)(2,1)}, u32[]{:S(2)}, u32[]{:S(2)}) async-start(bf16[8,800,320]{1,2,0:T(8,128)(2,1)} %copy.40), calls=%async_computation | async-start | bytes 9175040 | tf_op jit(solution)/shard_map/all_to_all | solution.py:84
  31.2 66.7 %all-gather = bf16[8,320,20]{1,2,0:T(8,128)(2,1)S(1)} all-gather(bf16[1,320,20]{1,2,0:T(8,128)(2,1)S(1)} %bitcast.39), channel_id=1, replica_groups=mesh['group'=8,'head'=4] {'group'}, dimensions={0}, use_global_device_ids=true | all-gather | bytes 115200 | tf_op jit(solution)/shard_map/all_gather | solution.py:47
  98.0 0.1 reshape.102
  98.1 0.1 add.116
  98.2 0.1 fusion.9
  98.4 0.2 multiply_exponential_fusion
  98.7 1.6 fusion.2
  100.4 16.8 %all-gather.6.cloned.1.call-done = bf16[2560,1280]{1,0:T(8,128)(2,1)} async-done(((bf16[320,1280]{1,0:T(8,128)(2,1)}), bf16[2560,1280]{1,0:T(8,128)(2,1)}) %all-gather.6.cloned.1.call-update) | async-done | bytes 6553616 | tf_op jit(solution)/shard_map/all_gather | solution.py:45
  117.2 3.9 %fusion.1 = bf16[16,1,1280]{2,0,1:T(8,128)(2,1)S(1)} fusion(bf16[2560,1280]{1,0:T(8,128)(2,1)} %all-gather.6.cloned.1.call-done, bf16[16,2560]{1,0:T(8,128)(2,1)S(1)} %copy-done.2, f32[2560]{0:T(1024)S(1)} %copy-done.6, f32[16]{0:T(128)S(1)} %add_rsqrt_fusion.2), kind=kOutput, calls=%fused_computation.4 | convolution fusion | flops 105041920 | bytes 6686784 | tf_op jit(solution)/shard_map/dot_general | solution.py:53
  121.1 0.1 reduce_sum.85
  121.2 0.1 broadcast_multiply_fusion
  121.3 8.4 %multiply_add_fusion = f32[16,20,64,128]{3,2,1,0:T(8,128)S(1)} fusion(f32[16,20,64,128]{3,2,1,0:T(8,128)} %param.23, f32[16,128]{1,0:T(8,128)S(1)} %get-tuple-element.19, f32[16,20,64]{2,1,0:T(8,128)S(1)} %broadcast_multiply_fusion, f32[16,20]{1,0:T(8,128)S(1)} %get-tuple-element.22), kind=kLoop, calls=%fused_computation | loop fusion | flops 7864320 | bytes 21062912 | tf_op jit(solution)/shard_map/add | solution.py:67
  129.8 4.1 %copy-done = f32[16,20,64,128]{3,2,1,0:T(8,128)} copy-done((f32[16,20,64,128]{3,2,1,0:T(8,128)}, f32[16,20,64,128]{3,2,1,0:T(8,128)S(1)}, u32[]{:S(2)}) %copy-start) | copy-done | bytes 10485784
  133.8 24.6 %fusion.21 = f32[16,1,20,64]{3,1,2,0:T(1,128)S(1)} fusion(f32[16,20,64,128]{3,2,1,0:T(8,128)S(1)} %multiply_add_fusion, f32[16,128,1,1]{1,2,3,0:T(1,128)S(1)} %bitcast.38), kind=kOutput, calls=%fused_computation.48 | convolution fusion | flops 31457280 | bytes 10575872 | tf_op jit(solution)/shard_map/shpn,sn->shp/dot_general | solution.py:68
  158.4 0.1 bitcast_add_fusion
  158.5 0.1 reshape.100
  158.6 7.0 %all-gather.10.cloned.1.call-done = bf16[2560,1280]{1,0:T(8,128)(2,1)} async-done(((bf16[320,1280]{1,0:T(8,128)(2,1)}), bf16[2560,1280]{1,0:T(8,128)(2,1)}) %all-gather.10.cloned.1.call-update) | async-done | bytes 6553616 | tf_op jit(solution)/shard_map/all_gather | solution.py:44
  165.6 4.0 %multiply_reduce_fusion.2 = (f32[16]{0:T(128)S(1)}, f32[16,1280]{1,0:T(8,128)S(1)}) fusion(f32[16,1280]{1,0:T(8,128)S(1)} %reshape.100, bf16[2560,1280]{1,0:T(8,128)(2,1)} %all-gather.10.cloned.1.call-done, bf16[16,2560]{1,0:T(8,128)(2,1)S(1)} %copy-done.2, f32[2560]{0:T(1024)S(1)} %copy-done.6, f32[16]{0:T(128)S(1)} %add_rsqrt_fusion.2), kind=kOutput, calls=%fused_computation.31 | convolution fusion | flops 105205744 | bytes 6809728 | tf_op jit(solution)/shard_map/dot_general | solution.py:52
  169.6 11.7 %psum.42 = f32[16]{0:T(128)S(1)} all-reduce(f32[16]{0:T(128)S(1)} %get-tuple-element.24), channel_id=1, replica_groups=mesh['group'=8,'head'=4] {'head'}, use_global_device_ids=true, to_apply=%region_6.7 | all-reduce | flops 16 | bytes 128 | tf_op jit(solution)/shard_map/psum | solution.py:73
  181.3 32.6 %all-gather.12.cloned.1.call-done = bf16[2560,1280]{1,0:T(8,128)(2,1)} async-done(((bf16[320,1280]{1,0:T(8,128)(2,1)}), bf16[2560,1280]{1,0:T(8,128)(2,1)}) %all-gather.12.cloned.1.call-update) | async-done | bytes 6553616 | tf_op jit(solution)/shard_map/all_gather | solution.py:48
  213.9 5.4 %fusion.12 = f32[16,2560]{1,0:T(8,128)} fusion(bf16[2560,1280]{1,0:T(8,128)(2,1)} %all-gather.12.cloned.1.call-done, f32[16,1280]{1,0:T(8,128)S(1)} %get-tuple-element.25, f32[1280]{0:T(1024)S(1)} %copy-done.11, f32[16]{0:T(128)S(1)} %add_rsqrt_fusion.1), kind=kOutput, calls=%fused_computation.34 | convolution fusion | flops 104919040 | bytes 6804544 | tf_op jit(solution)/shard_map/dot_general | solution.py:78
  219.3 35.0 %all-reduce.4.cloned.1.call-done = f32[16,2560]{1,0:T(8,128)} async-done(((f32[16,2560]{1,0:T(8,128)}), f32[16,2560]{1,0:T(8,128)}) %all-reduce.4.cloned.1.call-update) | async-done | bytes 163856 | tf_op jit(solution)/shard_map/psum | solution.py:81
  254.3 1.0 multiply_reduce_fusion.1
  255.3 1.0 multiply_convert_fusion
  256.3 10.0 %all_gather.23 = bf16[128,2560]{1,0:T(8,128)(2,1)S(1)} all-gather(bf16[16,2560]{1,0:T(8,128)(2,1)S(1)} %multiply_convert_fusion), channel_id=1, replica_groups=mesh['group'=8,'head'=4] {'group'}, dimensions={0}, use_global_device_ids=true | all-gather | bytes 737280 | tf_op jit(solution)/shard_map/all_gather | solution.py:86
  266.4 3.9 %fusion.22 = f32[8,16,800]{2,1,0:T(8,128)} fusion(bf16[8,16,2560]{2,1,0:T(8,128)(2,1)S(1)} %bitcast.37, bf16[800,2560,1]{0,1,2:T(8,128)(2,1)} %bitcast.9), kind=kOutput, calls=%fused_computation.49 | convolution fusion | flops 524288000 | bytes 5160960 | tf_op jit(solution)/shard_map/dot_general | solution.py:85
  270.3 3.5 %all-to-all-start.1 = ((f32[8,16,800]{2,1,0:T(8,128)}), f32[8,16,800]{2,1,0:T(8,128)S(1)}, u32[]{:S(2)}, u32[]{:S(2)}) async-start(f32[8,16,800]{2,1,0:T(8,128)} %fusion.22), calls=%async_computation.1 | async-start | bytes 917504 | tf_op jit(solution)/shard_map/all_to_all | solution.py:91
  273.8 0.2 reduce_max.23
  274.0 8.8 %all-to-all-done.1 = f32[8,16,800]{2,1,0:T(8,128)S(1)} async-done(((f32[8,16,800]{2,1,0:T(8,128)}), f32[8,16,800]{2,1,0:T(8,128)S(1)}, u32[]{:S(2)}, u32[]{:S(2)}) %all-to-all-start.1) | async-done | bytes 409632 | tf_op jit(solution)/shard_map/all_to_all | solution.py:91
  282.7 0.1 copy.42
  282.9 0.2 reduce_max.25
  283.1 0.2 all_to_all.32
  283.2 10.6 %all-reduce.1 = (f32[16]{0:T(128)S(1)}, f32[16]{0:T(128)S(1)}) all-reduce(bf16[16]{0:T(256)(128)(2,1)S(1)} %reduce_max.23, f32[16]{0:T(128)S(1)} %reduce_max.25), channel_id=1, replica_groups=mesh['group'=8,'head'=4] {'head'}, use_global_device_ids=true, to_apply=%region_4.5 | all-reduce | flops 32 | bytes 224 | tf_op jit(solution)/shard_map/pmax | solution.py:97
  293.9 0.3 fusion.8
  294.2 0.3 select_reduce_fusion
  294.5 8.5 %all-reduce = (f32[16]{0:T(128)S(1)}, f32[16]{0:T(128)S(1)}, f32[16]{0:T(128)S(1)}, f32[16]{0:T(128)S(1)}) all-reduce(f32[16]{0:T(128)S(1)} %get-tuple-element.11, f32[16]{0:T(128)S(1)} %get-tuple-element.10, f32[16]{0:T(128)S(1)} %get-tuple-element.9, f32[16]{0:T(128)S(1)} %get-tuple-element.8), channel_id=1, replica_groups=mesh['group'=8,'head'=4] {'head'}, use_global_device_ids=true, to_apply=%region_12.13 | all-reduce | flops 64 | bytes 512 | tf_op jit(solution)/shard_map/psum | solution.py:101
  303.0 0.5 fusion.15
  303.6 6.7 %copy.53 = bf16[2560,1280]{1,0:T(8,128)(2,1)} copy(bf16[2560,1280]{1,0:T(8,128)(2,1)} %all-gather.10.cloned.1.call-done) | data formatting | bytes 13107200
  310.3 3.3 %copy.54 = bf16[2560,1280]{1,0:T(8,128)(2,1)} copy(bf16[2560,1280]{1,0:T(8,128)(2,1)S(1)} %bitcast.33) | data formatting | bytes 13107200
  313.6 1.1 copy.55
  314.7 0.4 slice-done.3
  315.1 2.8 copy.56
  (64 shorter events, 0.5 us)
Async XLA Ops:
  7.2 91.5 %all-gather.8.cloned.1.call-start = ((), (), s32[]{:S(2)}) async-start(), calls=%async_computation.3 | async-start | bytes 1474560 | tf_op jit(solution)/shard_map/all_gather | solution.py:46
  7.9 109.3 %all-gather.6.cloned.1.call-start = ((), (), s32[]{:S(2)}) async-start(), calls=%async_computation.2 | async-start | bytes 7372800 | tf_op jit(solution)/shard_map/all_gather | solution.py:45
  8.7 157.0 %all-gather.10.cloned.1.call-start = ((), (), s32[]{:S(2)}) async-start(), calls=%async_computation.4 | async-start | bytes 7372800 | tf_op jit(solution)/shard_map/all_gather | solution.py:44
  9.4 204.5 %all-gather.12.cloned.1.call-start = ((), (), s32[]{:S(2)}) async-start(), calls=%async_computation.5 | async-start | bytes 7372800 | tf_op jit(solution)/shard_map/all_gather | solution.py:48
  25.7 5.5 %copy-start.9 = (bf16[320,20]{0,1:T(8,128)(2,1)S(1)}, bf16[320,20]{0,1:T(8,128)(2,1)}, u32[]{:S(2)}) copy-start(bf16[320,20]{0,1:T(8,128)(2,1)} %param.31) | copy-start | bytes 38404
  25.7 72.4 %copy-start.17 = (f32[20]{0:T(128)S(1)}, f32[20]{0:T(128)}, u32[]{:S(2)}) copy-start(f32[20]{0:T(128)} %param.39) | copy-start | bytes 244
  25.7 72.4 %copy-start.12 = (f32[1280]{0:T(1024)S(1)}, f32[1280]{0:T(1024)}, u32[]{:S(2)}) copy-start(f32[1280]{0:T(1024)} %param.35) | copy-start | bytes 15364
  25.7 72.5 %copy-start.2 = (bf16[16,2560]{1,0:T(8,128)(2,1)S(1)}, bf16[16,2560]{1,0:T(8,128)(2,1)}, u32[]{:S(2)}) copy-start(bf16[16,2560]{1,0:T(8,128)(2,1)} %param.22) | copy-start | bytes 245764
  25.7 72.6 %copy-start.6 = (f32[2560]{0:T(1024)S(1)}, f32[2560]{0:T(1024)}, u32[]{:S(2)}) copy-start(f32[2560]{0:T(1024)} %param.41) | copy-start | bytes 30724
  25.7 72.6 %copy-start.18 = (f32[20]{0:T(128)S(1)}, f32[20]{0:T(128)}, u32[]{:S(2)}) copy-start(f32[20]{0:T(128)} %param.38) | copy-start | bytes 244
  25.8 74.5 %copy-start.7 = (bf16[16,3,256]{2,0,1:T(8,128)(2,1)S(1)}, bf16[16,3,256]{2,0,1:T(8,128)(2,1)}, u32[]{:S(2)}) copy-start(bf16[16,3,256]{2,0,1:T(8,128)(2,1)} %param.25) | copy-start | bytes 73732
  25.8 74.5 %copy-start.13 = (f32[4,256]{1,0:T(4,128)S(1)}, f32[4,256]{1,0:T(4,128)}, u32[]{:S(2)}) copy-start(f32[4,256]{1,0:T(4,128)} %param.36) | copy-start | bytes 12292
  25.8 74.5 %copy-start.14 = (f32[256]{0:T(256)S(1)}, f32[256]{0:T(256)}, u32[]{:S(2)}) copy-start(f32[256]{0:T(256)} %param.37) | copy-start | bytes 3076
  25.8 240.6 %all-to-all-start = ((bf16[8,800,320]{1,2,0:T(8,128)(2,1)}), bf16[8,800,320]{1,2,0:T(8,128)(2,1)}, u32[]{:S(2)}, u32[]{:S(2)}) async-start(bf16[8,800,320]{1,2,0:T(8,128)(2,1)} %copy.40), calls=%async_computation | async-start | bytes 9175040 | tf_op jit(solution)/shard_map/all_to_all | solution.py:84
  31.2 89.9 %copy-start.4 = (bf16[16,3,1280]{2,0,1:T(8,128)(2,1)S(1)}, bf16[16,3,1280]{2,0,1:T(8,128)(2,1)}, u32[]{:S(2)}) copy-start(bf16[16,3,1280]{2,0,1:T(8,128)(2,1)} %param.24) | copy-start | bytes 368644
  31.2 89.9 %copy-start.8 = (f32[4,1280]{1,0:T(4,128)S(1)}, f32[4,1280]{1,0:T(4,128)}, u32[]{:S(2)}) copy-start(f32[4,1280]{1,0:T(4,128)} %param.34) | copy-start | bytes 61444
  31.2 223.1 %all-reduce.4.cloned.1.call-start = ((), (), s32[]{:S(2)}) async-start(), calls=%async_computation.6 | async-start | bytes 327680 | tf_op jit(solution)/shard_map/psum | solution.py:81
  98.1 31.6 %copy-start.5 = (bf16[2560,20]{0,1:T(8,128)(2,1)}, bf16[2560,20]{0,1:T(8,128)(2,1)S(1)}, u32[]{:S(2)}) copy-start(bf16[2560,20]{0,1:T(8,128)(2,1)S(1)} %reshape.102) | copy-start | bytes 307204
  129.7 4.1 %copy-start = (f32[16,20,64,128]{3,2,1,0:T(8,128)}, f32[16,20,64,128]{3,2,1,0:T(8,128)S(1)}, u32[]{:S(2)}) copy-start(f32[16,20,64,128]{3,2,1,0:T(8,128)S(1)} %multiply_add_fusion) | copy-start | bytes 31457284
  129.8 28.7 %copy-start.15 = (f32[20]{0:T(128)S(1)}, f32[20]{0:T(128)}, u32[]{:S(2)}) copy-start(f32[20]{0:T(128)} %param.40) | copy-start | bytes 244
  133.8 80.1 %copy-start.11 = (f32[1280]{0:T(1024)S(1)}, f32[1280]{0:T(1024)}, u32[]{:S(2)}) copy-start(f32[1280]{0:T(1024)} %param.42) | copy-start | bytes 15364
  158.6 96.7 %copy-start.10 = (f32[2560]{0:T(1024)S(1)}, f32[2560]{0:T(1024)}, u32[]{:S(2)}) copy-start(f32[2560]{0:T(1024)} %param.43) | copy-start | bytes 30724
  213.9 59.9 %copy-start.3 = (bf16[16,6400]{1,0:T(8,128)(2,1)S(1)}, bf16[16,6400]{1,0:T(8,128)(2,1)}, u32[]{:S(2)}) copy-start(bf16[16,6400]{1,0:T(8,128)(2,1)} %param.27) | copy-start | bytes 614404
  219.3 74.9 %copy-start.16 = (s32[16]{0:T(128)S(1)}, s32[16]{0:T(128)}, u32[]{:S(2)}) copy-start(s32[16]{0:T(128)} %param.26) | copy-start | bytes 196
  270.3 12.4 %all-to-all-start.1 = ((f32[8,16,800]{2,1,0:T(8,128)}), f32[8,16,800]{2,1,0:T(8,128)S(1)}, u32[]{:S(2)}, u32[]{:S(2)}) async-start(f32[8,16,800]{2,1,0:T(8,128)} %fusion.22), calls=%async_computation.1 | async-start | bytes 917504 | tf_op jit(solution)/shard_map/all_to_all | solution.py:91
  293.9 16.4 %slice-start = ((s8[6553600]{0:T(1024)(128)(4,1)}), s8[2359296]{0:T(1024)(128)(4,1)S(1)}, s32[]{:S(2)}) async-start(s8[6553600]{0:T(1024)(128)(4,1)} %bitcast.32), calls=%async_computation.7 | async-start | bytes 4718592
  303.6 6.7 %slice-start.1 = ((s8[6553600]{0:T(1024)(128)(4,1)}), s8[4194304]{0:T(1024)(128)(4,1)S(1)}, s32[]{:S(2)}) async-start(s8[6553600]{0:T(1024)(128)(4,1)} %bitcast.32), calls=%async_computation.8 | async-start | bytes 8388608
  303.6 11.1 %slice-start.2 = ((s8[6553600]{0:T(1024)(128)(4,1)}), s8[4194304]{0:T(1024)(128)(4,1)S(1)}, s32[]{:S(2)}) async-start(s8[6553600]{0:T(1024)(128)(4,1)} %bitcast.34), calls=%async_computation.9 | async-start | bytes 8388608
  310.3 3.3 %copy-start.1 = (bf16[2560,256]{1,0:T(8,128)(2,1)S(1)}, bf16[2560,256]{1,0:T(8,128)(2,1)}, u32[]{:S(2)}) copy-start(bf16[2560,256]{1,0:T(8,128)(2,1)} %all-gather.8.cloned.1.call-done) | copy-start | bytes 3932164
  310.3 4.8 %slice-start.3 = ((s8[6553600]{0:T(1024)(128)(4,1)}), s8[2359296]{0:T(1024)(128)(4,1)S(1)}, s32[]{:S(2)}) async-start(s8[6553600]{0:T(1024)(128)(4,1)} %bitcast.34), calls=%async_computation.10 | async-start | bytes 4718592
Sparse Core Ops, SparseCore 0:
  9.9 28.3 all-gather.7
  40.1 77.0 all-gather.5
  119.1 46.4 all-gather.9
  167.4 46.4 all-gather.11
  219.4 34.8 all-reduce.3
where the time goes:
time: 325 us; the launch traced here: 324 us
  blocking collectives  108 us (33%)
  waiting for transfers between devices  103 us (32%)
  matrix products  43.6 us (13%)
  local copies, waits for them, and re-layouts  34.9 us (11%)
  between operations  14.1 us (4%)
  other arithmetic  12.4 us (4%)
  starting transfers between devices  9.02 us (3%)
    all_gather x1, blocking collectives, shards(): lax.all_gather(in_dt, 'group', axis=0, tiled=True)  66.7 us
    psum x1, waiting for transfers between devices, shards(): mixed = lax.psum(partial_mix, 'head')  35 us
    all_gather x1, waiting for transfers between devices, shards(): lax.all_gather(out_t, 'group', axis=0, tiled=True)  32.6 us
    dot_general x1, matrix products, shards(): jnp.einsum('shpn,sn->shp', new_state, c_vals, precision=lax.Precision.HIG...  24.6 us
    unnamed x51, local copies, waits for them, and re-layouts  18.6 us
    all_gather x1, waiting for transfers between devices, shards(): lax.all_gather(in_x, 'group', axis=0, tiled=True)  16.8 us
    all_to_all x2, local copies, waits for them, and re-layouts, shards(): lax.all_to_all(lm_head, 'group', split_axis=0, concat_axis=1, tiled=True)  15.8 us
    psum x1, blocking collectives, shards(): square_total = lax.psum(jnp.sum(gated * gated, axis=-1), 'head')  11.7 us
  transfers between devices with their start and end apart: 7, of which 5 were waited for; matrix products, arithmetic and copies ran while one was open for 17% of the time, Pallas kernels for 0%

commit v1 on v0

--- a/solution.py
+++ b/solution.py
@@ -78,7 +78,7 @@
     partial_mix = lax.dot_general(
         gated_out, roll_out, (((1,), (1,)), ((), ())), preferred_element_type=jnp.float32
     )
-    mixed = lax.psum(partial_mix, "head")
+    mixed = jnp.sum(lax.all_gather(partial_mix, "head"), axis=0)
     final_hidden = rms_norm(stream_in + mixed, final_gain).astype(jnp.bfloat16)
     vocab_local = lm_head.shape[0]
     whole_rows = lax.all_to_all(lm_head, "group", split_axis=0, concat_axis=1, tiled=True)

time: 325 us -> 306 us (0.942)
  waiting for transfers between devices: 103 us -> 67.8 us
  blocking collectives: 108 us -> 126 us
    psum x1 -> x0, waiting for transfers between devices: 35 us -> none  [shards(): mixed = lax.psum(partial_mix, 'head')]
    all_gather x0 -> x1, blocking collectives: none -> 18.3 us  [shards(): mixed = jnp.sum(lax.all_gather(partial_mix, 'head'), axis=0)]
  transfers between devices with their start and end apart: 7 -> 6, of which waited for: 5 -> 4; matrix products, arithmetic and copies ran while one was open for 17% -> 18% of each run, Pallas kernels for 0% -> 0%
where the time goes in v1:
time: 306 us; the launch traced here: 305 us
  blocking collectives  126 us (41%)
  waiting for transfers between devices  67.8 us (22%)
  matrix products  42.9 us (14%)
  local copies, waits for them, and re-layouts  34.9 us (11%)
  between operations  14.1 us (5%)
  other arithmetic  10.6 us (3%)
  starting transfers between devices  8.98 us (3%)
    all_gather x1, blocking collectives, shards(): lax.all_gather(in_dt, 'group', axis=0, tiled=True)  66.8 us
    all_gather x1, waiting for transfers between devices, shards(): lax.all_gather(out_t, 'group', axis=0, tiled=True)  32.6 us
    dot_general x1, matrix products, shards(): jnp.einsum('shpn,sn->shp', new_state, c_vals, precision=lax.Precision.HIG...  24.6 us
    unnamed x51, local copies, waits for them, and re-layouts  18.6 us
    all_gather x1, blocking collectives, shards(): mixed = jnp.sum(lax.all_gather(partial_mix, 'head'), axis=0)  18.3 us
    all_gather x1, waiting for transfers between devices, shards(): lax.all_gather(in_x, 'group', axis=0, tiled=True)  16.8 us
    all_to_all x2, local copies, waits for them, and re-layouts, shards(): lax.all_to_all(lm_head, 'group', split_axis=0, concat_axis=1, tiled=True)  15.8 us
    psum x1, blocking collectives, shards(): square_total = lax.psum(jnp.sum(gated * gated, axis=-1), 'head')  11.7 us
  transfers between devices with their start and end apart: 6, of which 4 were waited for; matrix products, arithmetic and copies ran while one was open for 18% of the time, Pallas kernels for 0%

profile of v1, /device:TPU:0, one launch (start us, length us, event | category | flops | bytes accessed | tf_op | source)
XLA Modules:
  0.0 305.5 jit_solution(9979581910576380910)
XLA Ops:
  7.2 0.7 all-gather.9.cloned.1.call-update
  7.9 0.7 all-gather.7.cloned.1.call-update
  8.7 0.7 all-gather.11.cloned.1.call-update
  9.4 0.5 all-gather.13.cloned.1.call-update
  10.0 10.6 %all_to_all.26 = bf16[8,800,320]{1,0,2:T(8,128)(2,1)} reshape(bf16[6400,320]{0,1:T(8,128)(2,1)} %param.33) | data formatting | bytes 8192000 | tf_op jit(solution)/shard_map/all_to_all | solution.py:84
  20.5 5.2 %copy.40 = bf16[8,800,320]{1,2,0:T(8,128)(2,1)} copy(bf16[8,800,320]{1,0,2:T(8,128)(2,1)} %all_to_all.26) | data formatting | bytes 8192000 | tf_op jit(solution)/shard_map/all_to_all | solution.py:84
  25.8 5.4 %all-to-all-start = ((bf16[8,800,320]{1,2,0:T(8,128)(2,1)}), bf16[8,800,320]{1,2,0:T(8,128)(2,1)}, u32[]{:S(2)}, u32[]{:S(2)}) async-start(bf16[8,800,320]{1,2,0:T(8,128)(2,1)} %copy.40), calls=%async_computation | async-start | bytes 9175040 | tf_op jit(solution)/shard_map/all_to_all | solution.py:84
  31.2 66.8 %all-gather.1 = bf16[8,320,20]{1,2,0:T(8,128)(2,1)S(1)} all-gather(bf16[1,320,20]{1,2,0:T(8,128)(2,1)S(1)} %bitcast.41), channel_id=1, replica_groups=mesh['group'=8,'head'=4] {'group'}, dimensions={0}, use_global_device_ids=true | all-gather | bytes 115200 | tf_op jit(solution)/shard_map/all_gather | solution.py:47
  98.0 0.1 reshape.103
  98.1 0.1 add.114
  98.2 0.1 fusion.9
  98.4 0.2 multiply_exponential_fusion
  98.7 1.6 fusion.2
  100.4 16.8 %all-gather.7.cloned.1.call-done = bf16[2560,1280]{1,0:T(8,128)(2,1)} async-done(((bf16[320,1280]{1,0:T(8,128)(2,1)}), bf16[2560,1280]{1,0:T(8,128)(2,1)}) %all-gather.7.cloned.1.call-update) | async-done | bytes 6553616 | tf_op jit(solution)/shard_map/all_gather | solution.py:45
  117.2 3.9 %fusion.1 = bf16[16,1,1280]{2,0,1:T(8,128)(2,1)S(1)} fusion(bf16[2560,1280]{1,0:T(8,128)(2,1)} %all-gather.7.cloned.1.call-done, bf16[16,2560]{1,0:T(8,128)(2,1)S(1)} %copy-done.2, f32[2560]{0:T(1024)S(1)} %copy-done.6, f32[16]{0:T(128)S(1)} %add_rsqrt_fusion.2), kind=kOutput, calls=%fused_computation.4 | convolution fusion | flops 105041920 | bytes 6686784 | tf_op jit(solution)/shard_map/dot_general | solution.py:53
  121.1 0.1 reduce_sum.94
  121.2 0.1 broadcast_multiply_fusion
  121.3 8.4 %multiply_add_fusion = f32[16,20,64,128]{3,2,1,0:T(8,128)S(1)} fusion(f32[16,20,64,128]{3,2,1,0:T(8,128)} %param.23, f32[16,128]{1,0:T(8,128)S(1)} %get-tuple-element.19, f32[16,20,64]{2,1,0:T(8,128)S(1)} %broadcast_multiply_fusion, f32[16,20]{1,0:T(8,128)S(1)} %get-tuple-element.22), kind=kLoop, calls=%fused_computation | loop fusion | flops 7864320 | bytes 21062912 | tf_op jit(solution)/shard_map/add | solution.py:67
  129.8 4.1 %copy-done = f32[16,20,64,128]{3,2,1,0:T(8,128)} copy-done((f32[16,20,64,128]{3,2,1,0:T(8,128)}, f32[16,20,64,128]{3,2,1,0:T(8,128)S(1)}, u32[]{:S(2)}) %copy-start) | copy-done | bytes 10485784
  133.8 24.6 %fusion.21 = f32[16,1,20,64]{3,1,2,0:T(1,128)S(1)} fusion(f32[16,20,64,128]{3,2,1,0:T(8,128)S(1)} %multiply_add_fusion, f32[16,128,1,1]{1,2,3,0:T(1,128)S(1)} %bitcast.40), kind=kOutput, calls=%fused_computation.48 | convolution fusion | flops 31457280 | bytes 10575872 | tf_op jit(solution)/shard_map/shpn,sn->shp/dot_general | solution.py:68
  158.4 0.1 bitcast_add_fusion
  158.5 0.1 reshape.100
  158.6 7.0 %all-gather.11.cloned.1.call-done = bf16[2560,1280]{1,0:T(8,128)(2,1)} async-done(((bf16[320,1280]{1,0:T(8,128)(2,1)}), bf16[2560,1280]{1,0:T(8,128)(2,1)}) %all-gather.11.cloned.1.call-update) | async-done | bytes 6553616 | tf_op jit(solution)/shard_map/all_gather | solution.py:44
  165.6 4.0 %multiply_reduce_fusion.2 = (f32[16]{0:T(128)S(1)}, f32[16,1280]{1,0:T(8,128)S(1)}) fusion(f32[16,1280]{1,0:T(8,128)S(1)} %reshape.100, bf16[2560,1280]{1,0:T(8,128)(2,1)} %all-gather.11.cloned.1.call-done, bf16[16,2560]{1,0:T(8,128)(2,1)S(1)} %copy-done.2, f32[2560]{0:T(1024)S(1)} %copy-done.6, f32[16]{0:T(128)S(1)} %add_rsqrt_fusion.2), kind=kOutput, calls=%fused_computation.31 | convolution fusion | flops 105205744 | bytes 6809728 | tf_op jit(solution)/shard_map/dot_general | solution.py:52
  169.6 11.7 %psum.35 = f32[16]{0:T(128)S(1)} all-reduce(f32[16]{0:T(128)S(1)} %get-tuple-element.24), channel_id=1, replica_groups=mesh['group'=8,'head'=4] {'head'}, use_global_device_ids=true, to_apply=%region_6.7 | all-reduce | flops 16 | bytes 128 | tf_op jit(solution)/shard_map/psum | solution.py:73
  181.3 32.6 %all-gather.13.cloned.1.call-done = bf16[2560,1280]{1,0:T(8,128)(2,1)} async-done(((bf16[320,1280]{1,0:T(8,128)(2,1)}), bf16[2560,1280]{1,0:T(8,128)(2,1)}) %all-gather.13.cloned.1.call-update) | async-done | bytes 6553616 | tf_op jit(solution)/shard_map/all_gather | solution.py:48
  213.9 4.7 %fusion.12 = f32[16,2560]{1,0:T(8,128)S(1)} fusion(bf16[2560,1280]{1,0:T(8,128)(2,1)} %all-gather.13.cloned.1.call-done, f32[16,1280]{1,0:T(8,128)S(1)} %get-tuple-element.25, f32[1280]{0:T(1024)S(1)} %copy-done.11, f32[16]{0:T(128)S(1)} %add_rsqrt_fusion.1), kind=kOutput, calls=%fused_computation.34 | convolution fusion | flops 104919040 | bytes 6804544 | tf_op jit(solution)/shard_map/dot_general | solution.py:78
  218.5 18.3 %all-gather = f32[64,2560]{1,0:T(8,128)S(1)} all-gather(f32[16,2560]{1,0:T(8,128)S(1)} %fusion.12), channel_id=2, replica_groups=mesh['group'=8,'head'=4] {'head'}, dimensions={0}, use_global_device_ids=true | all-gather | bytes 819200 | tf_op jit(solution)/shard_map/all_gather | solution.py:81
  236.8 0.1 multiply_reduce_fusion.1
  237.0 0.1 multiply_convert_fusion
  237.1 10.1 %all_gather.31 = bf16[128,2560]{1,0:T(8,128)(2,1)S(1)} all-gather(bf16[16,2560]{1,0:T(8,128)(2,1)S(1)} %multiply_convert_fusion), channel_id=1, replica_groups=mesh['group'=8,'head'=4] {'group'}, dimensions={0}, use_global_device_ids=true | all-gather | bytes 737280 | tf_op jit(solution)/shard_map/all_gather | solution.py:86
  247.2 3.9 %fusion.22 = f32[8,16,800]{2,1,0:T(8,128)} fusion(bf16[8,16,2560]{2,1,0:T(8,128)(2,1)S(1)} %bitcast.38, bf16[800,2560,1]{0,1,2:T(8,128)(2,1)} %bitcast.10), kind=kOutput, calls=%fused_computation.49 | convolution fusion | flops 524288000 | bytes 5160960 | tf_op jit(solution)/shard_map/dot_general | solution.py:85
  251.1 3.5 %all-to-all-start.1 = ((f32[8,16,800]{2,1,0:T(8,128)}), f32[8,16,800]{2,1,0:T(8,128)S(1)}, u32[]{:S(2)}, u32[]{:S(2)}) async-start(f32[8,16,800]{2,1,0:T(8,128)} %fusion.22), calls=%async_computation.1 | async-start | bytes 917504 | tf_op jit(solution)/shard_map/all_to_all | solution.py:91
  254.6 0.2 reduce_max.23
  254.8 8.8 %all-to-all-done.1 = f32[8,16,800]{2,1,0:T(8,128)S(1)} async-done(((f32[8,16,800]{2,1,0:T(8,128)}), f32[8,16,800]{2,1,0:T(8,128)S(1)}, u32[]{:S(2)}, u32[]{:S(2)}) %all-to-all-start.1) | async-done | bytes 409632 | tf_op jit(solution)/shard_map/all_to_all | solution.py:91
  263.5 0.1 copy.42
  263.7 0.2 reduce_max.25
  263.9 0.2 all_to_all.32
  264.0 10.9 %all-reduce.1 = (f32[16]{0:T(128)S(1)}, f32[16]{0:T(128)S(1)}) all-reduce(bf16[16]{0:T(256)(128)(2,1)S(1)} %reduce_max.23, f32[16]{0:T(128)S(1)} %reduce_max.25), channel_id=1, replica_groups=mesh['group'=8,'head'=4] {'head'}, use_global_device_ids=true, to_apply=%region_4.5 | all-reduce | flops 32 | bytes 224 | tf_op jit(solution)/shard_map/pmax | solution.py:97
  274.9 0.3 fusion.8
  275.3 0.3 select_reduce_fusion
  275.6 8.5 %all-reduce = (f32[16]{0:T(128)S(1)}, f32[16]{0:T(128)S(1)}, f32[16]{0:T(128)S(1)}, f32[16]{0:T(128)S(1)}) all-reduce(f32[16]{0:T(128)S(1)} %get-tuple-element.11, f32[16]{0:T(128)S(1)} %get-tuple-element.10, f32[16]{0:T(128)S(1)} %get-tuple-element.9, f32[16]{0:T(128)S(1)} %get-tuple-element.8), channel_id=1, replica_groups=mesh['group'=8,'head'=4] {'head'}, use_global_device_ids=true, to_apply=%region_12.13 | all-reduce | flops 64 | bytes 512 | tf_op jit(solution)/shard_map/psum | solution.py:101
  284.1 0.5 fusion.15
  284.6 6.7 %copy.52 = bf16[2560,1280]{1,0:T(8,128)(2,1)} copy(bf16[2560,1280]{1,0:T(8,128)(2,1)} %all-gather.11.cloned.1.call-done) | data formatting | bytes 13107200
  291.3 3.3 %copy.53 = bf16[2560,1280]{1,0:T(8,128)(2,1)} copy(bf16[2560,1280]{1,0:T(8,128)(2,1)S(1)} %bitcast.34) | data formatting | bytes 13107200
  294.7 1.1 copy.54
  295.7 0.4 slice-done.3
  296.1 2.8 copy.55
  (63 shorter events, 0.4 us)
Async XLA Ops:
  7.2 91.5 %all-gather.9.cloned.1.call-start = ((), (), s32[]{:S(2)}) async-start(), calls=%async_computation.3 | async-start | bytes 1474560 | tf_op jit(solution)/shard_map/all_gather | solution.py:46
  7.9 109.3 %all-gather.7.cloned.1.call-start = ((), (), s32[]{:S(2)}) async-start(), calls=%async_computation.2 | async-start | bytes 7372800 | tf_op jit(solution)/shard_map/all_gather | solution.py:45
  8.7 157.0 %all-gather.11.cloned.1.call-start = ((), (), s32[]{:S(2)}) async-start(), calls=%async_computation.4 | async-start | bytes 7372800 | tf_op jit(solution)/shard_map/all_gather | solution.py:44
  9.4 204.5 %all-gather.13.cloned.1.call-start = ((), (), s32[]{:S(2)}) async-start(), calls=%async_computation.5 | async-start | bytes 7372800 | tf_op jit(solution)/shard_map/all_gather | solution.py:48
  25.7 5.4 %copy-start.9 = (bf16[320,20]{0,1:T(8,128)(2,1)S(1)}, bf16[320,20]{0,1:T(8,128)(2,1)}, u32[]{:S(2)}) copy-start(bf16[320,20]{0,1:T(8,128)(2,1)} %param.31) | copy-start | bytes 38404
  25.7 72.4 %copy-start.17 = (f32[20]{0:T(128)S(1)}, f32[20]{0:T(128)}, u32[]{:S(2)}) copy-start(f32[20]{0:T(128)} %param.39) | copy-start | bytes 244
  25.7 72.4 %copy-start.12 = (f32[1280]{0:T(1024)S(1)}, f32[1280]{0:T(1024)}, u32[]{:S(2)}) copy-start(f32[1280]{0:T(1024)} %param.35) | copy-start | bytes 15364
  25.7 72.5 %copy-start.2 = (bf16[16,2560]{1,0:T(8,128)(2,1)S(1)}, bf16[16,2560]{1,0:T(8,128)(2,1)}, u32[]{:S(2)}) copy-start(bf16[16,2560]{1,0:T(8,128)(2,1)} %param.22) | copy-start | bytes 245764
  25.7 72.6 %copy-start.6 = (f32[2560]{0:T(1024)S(1)}, f32[2560]{0:T(1024)}, u32[]{:S(2)}) copy-start(f32[2560]{0:T(1024)} %param.41) | copy-start | bytes 30724
  25.7 72.6 %copy-start.18 = (f32[20]{0:T(128)S(1)}, f32[20]{0:T(128)}, u32[]{:S(2)}) copy-start(f32[20]{0:T(128)} %param.38) | copy-start | bytes 244
  25.8 74.5 %copy-start.7 = (bf16[16,3,256]{2,0,1:T(8,128)(2,1)S(1)}, bf16[16,3,256]{2,0,1:T(8,128)(2,1)}, u32[]{:S(2)}) copy-start(bf16[16,3,256]{2,0,1:T(8,128)(2,1)} %param.25) | copy-start | bytes 73732
  25.8 74.5 %copy-start.13 = (f32[4,256]{1,0:T(4,128)S(1)}, f32[4,256]{1,0:T(4,128)}, u32[]{:S(2)}) copy-start(f32[4,256]{1,0:T(4,128)} %param.36) | copy-start | bytes 12292
  25.8 74.5 %copy-start.14 = (f32[256]{0:T(256)S(1)}, f32[256]{0:T(256)}, u32[]{:S(2)}) copy-start(f32[256]{0:T(256)} %param.37) | copy-start | bytes 3076
  25.8 221.4 %all-to-all-start = ((bf16[8,800,320]{1,2,0:T(8,128)(2,1)}), bf16[8,800,320]{1,2,0:T(8,128)(2,1)}, u32[]{:S(2)}, u32[]{:S(2)}) async-start(bf16[8,800,320]{1,2,0:T(8,128)(2,1)} %copy.40), calls=%async_computation | async-start | bytes 9175040 | tf_op jit(solution)/shard_map/all_to_all | solution.py:84
  31.2 89.9 %copy-start.4 = (bf16[16,3,1280]{2,0,1:T(8,128)(2,1)S(1)}, bf16[16,3,1280]{2,0,1:T(8,128)(2,1)}, u32[]{:S(2)}) copy-start(bf16[16,3,1280]{2,0,1:T(8,128)(2,1)} %param.24) | copy-start | bytes 368644
  31.2 89.9 %copy-start.8 = (f32[4,1280]{1,0:T(4,128)S(1)}, f32[4,1280]{1,0:T(4,128)}, u32[]{:S(2)}) copy-start(f32[4,1280]{1,0:T(4,128)} %param.34) | copy-start | bytes 61444
  98.1 31.6 %copy-start.5 = (bf16[2560,20]{0,1:T(8,128)(2,1)}, bf16[2560,20]{0,1:T(8,128)(2,1)S(1)}, u32[]{:S(2)}) copy-start(bf16[2560,20]{0,1:T(8,128)(2,1)S(1)} %reshape.103) | copy-start | bytes 307204
  129.7 4.1 %copy-start = (f32[16,20,64,128]{3,2,1,0:T(8,128)}, f32[16,20,64,128]{3,2,1,0:T(8,128)S(1)}, u32[]{:S(2)}) copy-start(f32[16,20,64,128]{3,2,1,0:T(8,128)S(1)} %multiply_add_fusion) | copy-start | bytes 31457284
  129.8 28.7 %copy-start.15 = (f32[20]{0:T(128)S(1)}, f32[20]{0:T(128)}, u32[]{:S(2)}) copy-start(f32[20]{0:T(128)} %param.40) | copy-start | bytes 244
  133.8 80.1 %copy-start.11 = (f32[1280]{0:T(1024)S(1)}, f32[1280]{0:T(1024)}, u32[]{:S(2)}) copy-start(f32[1280]{0:T(1024)} %param.42) | copy-start | bytes 15364
  158.6 78.4 %copy-start.10 = (f32[2560]{0:T(1024)S(1)}, f32[2560]{0:T(1024)}, u32[]{:S(2)}) copy-start(f32[2560]{0:T(1024)} %param.43) | copy-start | bytes 30724
  218.5 36.0 %copy-start.3 = (bf16[16,6400]{1,0:T(8,128)(2,1)S(1)}, bf16[16,6400]{1,0:T(8,128)(2,1)}, u32[]{:S(2)}) copy-start(bf16[16,6400]{1,0:T(8,128)(2,1)} %param.27) | copy-start | bytes 614404
  236.8 38.5 %copy-start.16 = (s32[16]{0:T(128)S(1)}, s32[16]{0:T(128)}, u32[]{:S(2)}) copy-start(s32[16]{0:T(128)} %param.26) | copy-start | bytes 196
  251.1 12.4 %all-to-all-start.1 = ((f32[8,16,800]{2,1,0:T(8,128)}), f32[8,16,800]{2,1,0:T(8,128)S(1)}, u32[]{:S(2)}, u32[]{:S(2)}) async-start(f32[8,16,800]{2,1,0:T(8,128)} %fusion.22), calls=%async_computation.1 | async-start | bytes 917504 | tf_op jit(solution)/shard_map/all_to_all | solution.py:91
  274.9 16.4 %slice-start = ((s8[6553600]{0:T(1024)(128)(4,1)}), s8[2359296]{0:T(1024)(128)(4,1)S(1)}, s32[]{:S(2)}) async-start(s8[6553600]{0:T(1024)(128)(4,1)} %bitcast.33), calls=%async_computation.6 | async-start | bytes 4718592
  284.6 6.7 %slice-start.1 = ((s8[6553600]{0:T(1024)(128)(4,1)}), s8[4194304]{0:T(1024)(128)(4,1)S(1)}, s32[]{:S(2)}) async-start(s8[6553600]{0:T(1024)(128)(4,1)} %bitcast.33), calls=%async_computation.7 | async-start | bytes 8388608
  284.6 11.1 %slice-start.2 = ((s8[6553600]{0:T(1024)(128)(4,1)}), s8[4194304]{0:T(1024)(128)(4,1)S(1)}, s32[]{:S(2)}) async-start(s8[6553600]{0:T(1024)(128)(4,1)} %bitcast.35), calls=%async_computation.8 | async-start | bytes 8388608
  291.3 3.3 %copy-start.1 = (bf16[2560,256]{1,0:T(8,128)(2,1)S(1)}, bf16[2560,256]{1,0:T(8,128)(2,1)}, u32[]{:S(2)}) copy-start(bf16[2560,256]{1,0:T(8,128)(2,1)} %all-gather.9.cloned.1.call-done) | copy-start | bytes 3932164
  291.3 4.8 %slice-start.3 = ((s8[6553600]{0:T(1024)(128)(4,1)}), s8[2359296]{0:T(1024)(128)(4,1)S(1)}, s32[]{:S(2)}) async-start(s8[6553600]{0:T(1024)(128)(4,1)} %bitcast.35), calls=%async_computation.9 | async-start | bytes 4718592
Sparse Core Ops, SparseCore 0:
  9.9 28.3 all-gather.8
  40.1 77.0 all-gather.6
  119.1 46.4 all-gather.10
  167.4 46.4 all-gather.12
